TPU v7x, 32 devices: a whole 2x2x4 slice. The times are simulated.
32 devices in a mesh: gx: 4 (over x, core), gy: 2 (over y), gz: 4 (over z).
Axes of the slice: x: 2, y: 2, z: 4, core: 2. Of those that a mesh axis runs over, the one named last changes fastest.
Arguments:
- node_feats: bfloat16 [64, 32, 128, 128], P('gx', 'gy', 'gz'), may hold values from -6 to 6
- node_type: int32 [64, 32, 128], P('gx', 'gy', 'gz'), may hold values from 0 to 3
- boundary_code: int32 [64, 32, 128], P('gx', 'gy', 'gz'), may hold values from 0 to 2
- wall_flag: int32 [64, 32, 128], P('gx', 'gy', 'gz'), may hold values from 0 to 1, as said below
- type_table: float32 [4, 128], replicated, may hold values from -3 to 3
- boundary_table: float32 [3, 128], replicated, may hold values from -3 to 3
- edge_self: bfloat16 [2, 128, 128], replicated, may hold values from -0.5 to 0.5
- edge_neighbour: bfloat16 [2, 128, 128], replicated, may hold values from -0.5 to 0.5
- edge_bias: float32 [2, 6, 128], replicated, may hold values from -3 to 3
- edge_out: bfloat16 [2, 128, 128], replicated, may hold values from -0.5 to 0.5
- node_self: bfloat16 [2, 128, 128], replicated, may hold values from -0.5 to 0.5
- node_aggregate: bfloat16 [2, 128, 128], replicated, may hold values from -0.5 to 0.5
- node_out: bfloat16 [2, 128, 128], replicated, may hold values from -0.5 to 0.5
- node_gain: float32 [2, 128], replicated, may hold values from 0.25 to 1.75
Outputs:
- latent: bfloat16 [64, 32, 128, 128], P('gx', 'gy', 'gz')
- wall_mean: float32 [128], replicated
Inputs may be any that keep to these rules, and one draw needn't show every extreme that they name: Every node whose wall-normal index is 0 or 31 has wall_flag 1.
All inputs are finite; a program needn't handle non-finite values.
Results may differ from a plain program's by a relative error of at most 0.012.
Values may be sent and summed in bfloat16 or wider, within the bound.
A program may use at most 128 MiB of HBM per device.

v0:
```python
import jax
import jax.numpy as jnp
from jax import lax
from jax.sharding import PartitionSpec as P

epsilon = 1e-05


def with_halo(block, sides, width):
    for axis, dim in sides:
        count = lax.axis_size(axis)
        forward = [(i, i + 1) for i in range(count - 1)]
        forward.append((count - 1, 0))
        backward = [(target, source) for source, target in forward]
        low = lax.ppermute(
            lax.slice_in_dim(block, block.shape[dim] - width, None, axis=dim), axis, forward
        )
        high = lax.ppermute(lax.slice_in_dim(block, 0, width, axis=dim), axis, backward)
        block = jnp.concatenate([low, block, high], axis=dim)
    return block


def lookup(codes, table):
    total = jnp.zeros(codes.shape + (table.shape[1],), jnp.float32)
    for entry in range(table.shape[0]):
        total = total + (codes == entry).astype(jnp.float32)[..., None] * table[entry]
    return total


def project(latent, weight):
    return jnp.dot(latent, weight, preferred_element_type=jnp.float32).astype(jnp.bfloat16)


def update_nodes(
    centre_latent,
    sendpart_wide,
    rows_y,
    total_y,
    which_layer,
    edge_self,
    edge_bias,
    edge_out,
    node_self,
    node_aggregate,
    node_out,
    node_gain,
):
    selfpart = jnp.dot(centre_latent, edge_self[which_layer], preferred_element_type=jnp.float32)
    lower_ok = (rows_y >= 1).astype(jnp.float32)[None, :, None, None]
    upper_ok = (rows_y < total_y - 1).astype(jnp.float32)[None, :, None, None]
    neighbours = [
        sendpart_wide[:-2, 1:-1, 1:-1],
        sendpart_wide[2:, 1:-1, 1:-1],
        sendpart_wide[1:-1, :-2, 1:-1],
        sendpart_wide[1:-1, 2:, 1:-1],
        sendpart_wide[1:-1, 1:-1, :-2],
        sendpart_wide[1:-1, 1:-1, 2:],
    ]
    masks = [None, None, lower_ok, upper_ok, None, None]
    aggregate = jnp.zeros(selfpart.shape, jnp.float32)
    for direction in range(6):
        hidden = jax.nn.silu(
            selfpart + neighbours[direction].astype(jnp.float32) + edge_bias[which_layer, direction]
        ).astype(jnp.bfloat16)
        message = jnp.dot(hidden, edge_out[which_layer], preferred_element_type=jnp.float32)
        if masks[direction] is not None:
            message = message * masks[direction]
        aggregate = aggregate + message
    aggregate = aggregate.astype(jnp.bfloat16)
    before = jnp.dot(
        centre_latent, node_self[which_layer], preferred_element_type=jnp.float32
    ) + jnp.dot(aggregate, node_aggregate[which_layer], preferred_element_type=jnp.float32)
    inner = jax.nn.silu(before).astype(jnp.bfloat16)
    update = jnp.dot(inner, node_out[which_layer], preferred_element_type=jnp.float32)
    centre = jnp.mean(update, axis=-1, keepdims=True)
    spread = jnp.mean(jnp.square(update - centre), axis=-1, keepdims=True)
    normed = (update - centre) * lax.rsqrt(spread + epsilon) * node_gain[which_layer]
    return (centre_latent.astype(jnp.float32) + normed).astype(jnp.bfloat16)


def per_device(
    node_feats,
    node_type,
    boundary_code,
    wall_flag,
    type_table,
    boundary_table,
    edge_self,
    edge_neighbour,
    edge_bias,
    edge_out,
    node_self,
    node_aggregate,
    node_out,
    node_gain,
):
    cells_y = node_feats.shape[1]
    total_y = cells_y * lax.axis_size("gy")
    first_y = lax.axis_index("gy") * cells_y
    layer_count = edge_self.shape[0]
    weights = (edge_self, edge_bias, edge_out, node_self, node_aggregate, node_out, node_gain)
    start_latent = (
        node_feats.astype(jnp.float32)
        + lookup(node_type, type_table)
        + lookup(boundary_code, boundary_table)
    ).astype(jnp.bfloat16)
    latent = start_latent
    rows_y = first_y + jnp.arange(cells_y, dtype=jnp.int32)
    for which_layer in range(layer_count):
        sendpart = project(latent, edge_neighbour[which_layer])
        padded = with_halo(sendpart, (("gx", 0), ("gy", 1), ("gz", 2)), 1)
        latent = update_nodes(latent, padded, rows_y, total_y, which_layer, *weights)
    flags = wall_flag.astype(jnp.bfloat16)
    wall_part = jnp.einsum("xyzh,xyz->h", latent, flags, preferred_element_type=jnp.float32)
    count_part = jnp.sum(wall_flag.astype(jnp.float32))
    wall_sum, wall_count = lax.psum((wall_part, count_part), ("gx", "gy", "gz"))
    return (latent, wall_sum / wall_count)


def solution(mesh):
    return jax.shard_map(
        per_device,
        mesh=mesh,
        in_specs=(
            P("gx", "gy", "gz", None),
            P("gx", "gy", "gz"),
            P("gx", "gy", "gz"),
            P("gx", "gy", "gz"),
            P(),
            P(),
            P(),
            P(),
            P(),
            P(),
            P(),
            P(),
            P(),
            P(),
        ),
        out_specs=(P("gx", "gy", "gz", None), P()),
        check_vma=False,
    )
```

profile of v0, /device:TPU:0, one launch (start us, length us, event | category | flops | bytes accessed | tf_op | source)
XLA Modules:
  0.0 176.6 jit_solution(13289279170880086438)
XLA Ops:
  0.6 1.1 compare_convert_fusion.2
  1.7 0.8 slice_bitcast_fusion.16
  2.6 9.9 %add_convert_fusion.4 = bf16[16,16,32,128]{3,2,1,0:T(8,128)(2,1)S(1)} fusion(bf16[16,16,32,128]{3,2,1,0:T(8,128)(2,1)} %param.14, f32[128]{0:T(128)S(1)} %get-tuple-element.40, f32[16,16,32]{2,1,0:T(8,128)S(1)} %get-tuple-element.21, f32[128]{0:T(128)S(1)} %get-tuple-element.41, f32[16,16,32]{2,1,0:T(8,128)S(1)} %get-tuple-element.22, ...), kind=kLoop, calls=%fused_computation.20 | loop fusion | flops 16777216 | bytes 4427264 | tf_op jit(solution)/shard_map/convert_element_type | solution.py:106
  12.5 0.7 convolution_convert_fusion.1
  13.2 1.3 copy-done
  14.6 0.7 fusion.98
  15.7 1.9 %collective-permute-start.1 = (bf16[1,16,32,128]{3,2,1,0:T(8,128)(2,1)S(1)}, bf16[1,16,32,128]{3,2,1,0:T(8,128)(2,1)S(1)}, u32[]{:S(2)}, u32[]{:S(2)}) collective-permute-start(bf16[1,16,32,128]{3,2,1,0:T(8,128)(2,1)S(1)} %get-tuple-element.15), channel_id=1, source_target_pairs={{8,0},{16,8},{24,16},{0,24},{9,1},{17,9},{25,17},{1,25},{10,2},{18... | collective-permute-start | bytes 393224 | tf_op jit(solution)/shard_map/ppermute | solution.py:18
  17.7 2.7 %fusion.31 = f32[16,16,32,128]{3,2,1,0:T(8,128)} fusion(bf16[16,16,32,128]{3,2,1,0:T(8,128)(2,1)S(1)} %add_convert_fusion.4, bf16[2,128,128]{2,1,0:T(8,128)(2,1)S(1)} %copy-done.7), kind=kOutput, calls=%fused_computation.118 | convolution fusion | flops 268435456 | bytes 6324224 | tf_op jit(solution)/shard_map/dot_general | solution.py:48
  20.9 3.5 %fusion.33 = f32[16,16,32,128]{3,2,1,0:T(8,128)} fusion(bf16[16,16,32,128]{3,2,1,0:T(8,128)(2,1)S(1)} %add_convert_fusion.4, bf16[2,128,128]{2,1,0:T(8,128)(2,1)} %param.24), kind=kOutput, calls=%fused_computation.120 | convolution fusion | flops 268435456 | bytes 6324224 | tf_op jit(solution)/shard_map/dot_general | solution.py:70
  24.4 1.3 slice_bitcast_fusion
  25.7 0.6 convert_bitcast_fusion
  26.4 0.7 convert_reduce_fusion
  27.1 1.0 pad_maximum_fusion.59
  28.1 2.4 %collective-permute-start.2 = (bf16[18,1,32,128]{3,2,1,0:T(8,128)(2,1)S(1)}, bf16[18,1,32,128]{3,2,1,0:T(8,128)(2,1)S(1)}, u32[]{:S(2)}, u32[]{:S(2)}) collective-permute-start(bf16[18,1,32,128]{3,2,1,0:T(8,128)(2,1)S(1)} %get-tuple-element.10), channel_id=1, source_target_pairs={{0,4},{4,0},{1,5},{5,1},{2,6},{6,2},{3,7},{7,3},{8,12},{12,8},{9,1... | collective-permute-start | bytes 442376 | tf_op jit(solution)/shard_map/ppermute | solution.py:15
  30.6 4.3 %fusion.6 = f32[16,16,32,128]{3,2,1,0:T(8,128)S(1)} fusion(f32[16,16,32,128]{3,2,1,0:T(8,128)} %fusion.31, bf16[16,16,32,128]{3,2,1,0:T(8,128)(2,1)} %copy-done, bf16[1,16,32,128]{3,2,1,0:T(8,128)(2,1)S(1)} %collective-permute-done, f32[128]{0:T(128)} %get-tuple-element.33, bf16[2,128,128]{2,1,0:T(8,128)(2,1)} %param.23), kind=kOutput, calls=%fused_computation.63 | convolution fusion | flops 277872640 | bytes 10650112 | tf_op jit(solution)/shard_map/dot_general | solution.py:65
  35.2 1.3 fusion.7
  36.5 1.2 collective-permute-done.3
  38.0 1.6 collective-permute-start.4
  39.6 2.3 %collective-permute-start.5 = (bf16[18,18,1,128]{3,2,1,0:T(2,128)(2,1)S(1)}, bf16[18,18,1,128]{3,2,1,0:T(2,128)(2,1)S(1)}, u32[]{:S(2)}, u32[]{:S(2)}) collective-permute-start(bf16[18,18,1,128]{3,2,1,0:T(2,128)(2,1)S(1)} %get-tuple-element.6), channel_id=1, source_target_pairs={{1,0},{2,1},{3,2},{0,3},{5,4},{6,5},{7,6},{4,7},{9,8},{10,9},{11,1... | collective-permute-start | bytes 248840 | tf_op jit(solution)/shard_map/ppermute | solution.py:18
  41.9 1.3 fusion.10
  43.2 2.9 %fusion.11 = f32[16,16,32,128]{3,2,1,0:T(8,128)} fusion(f32[16,16,32,128]{3,2,1,0:T(8,128)S(1)} %copy-done.4, bf16[18,1,32,128]{3,2,1,0:T(8,128)(2,1)S(1)} %collective-permute-done.3, bf16[1,16,32,128]{3,2,1,0:T(8,128)(2,1)S(1)} %collective-permute-done.1, bf16[16,16,32,128]{3,2,1,0:T(8,128)(2,1)S(1)} %copy-done.1, ...), kind=kOutput, calls=%fused_computation.68 | convolution fusion | flops 279969792 | bytes 10928640 | tf_op jit(solution)/shard_map/dot_general | solution.py:65
  46.2 0.9 collective-permute-done.4
  47.0 4.7 %fusion.14 = f32[16,16,32,128]{3,2,1,0:T(8,128)} fusion(f32[16,16,32,128]{3,2,1,0:T(8,128)S(1)} %copy-done.4, bf16[18,18,1,128]{3,2,1,0:T(2,128)(2,1)S(1)} %collective-permute-done.4, bf16[18,1,32,128]{3,2,1,0:T(8,128)(2,1)S(1)} %collective-permute-done.3, bf16[18,1,32,128]{3,2,1,0:T(8,128)(2,1)S(1)} %collective-permute-done.2, ...), kind=kOutput, calls=%fused_computation.71 | convolution fusion | flops 288358400 | bytes 11241984 | tf_op jit(solution)/shard_map/dot_general | solution.py:65
  51.7 7.8 %add_convert_fusion.3 = bf16[16,16,32,128]{3,2,1,0:T(8,128)(2,1)} fusion(f32[16,16,32,128]{3,2,1,0:T(8,128)} %fusion.14, f32[16,16,32,128]{3,2,1,0:T(8,128)} %fusion.11, f32[16,16,32,128]{3,2,1,0:T(8,128)S(1)} %fusion.10, f32[16,16,32,128]{3,2,1,0:T(8,128)S(1)} %fusion.6, f32[16,16,32,128]{3,2,1,0:T(8,128)S(1)} %fusion.7, ...), kind=kOutput, calls=%fused_computation.13 | convolution fusion | flops 296747008 | bytes 30117376 | tf_op jit(solution)/shard_map/dot_general | solution.py:65
  59.5 6.4 %fusion.99 = (f32[16,16,32]{2,1,0:T(8,128)S(1)}, f32[16,16,32,128]{3,2,1,0:T(8,128)}) fusion(bf16[2,128,128]{2,1,0:T(8,128)(2,1)S(1)} %copy-done.34, f32[16,16,32,128]{3,2,1,0:T(8,128)} %fusion.33, bf16[16,16,32,128]{3,2,1,0:T(8,128)(2,1)} %add_convert_fusion.3, bf16[2,128,128]{2,1,0:T(8,128)(2,1)S(1)} %copy-done.35), kind=kOutput, calls=%fused_computation.209 | convolution fusion | flops 544202752 | bytes 10584064 | tf_op jit(solution)/shard_map/dot_general | solution.py:74
  66.0 4.1 %multiply_reduce_fusion.1 = f32[16,16,32]{2,1,0:T(8,128)S(1)} fusion(f32[16,16,32,128]{3,2,1,0:T(8,128)} %get-tuple-element.45, f32[16,16,32]{2,1,0:T(8,128)S(1)} %broadcast_multiply_fusion.1), kind=kLoop, calls=%fused_computation.11 | loop fusion | flops 3137536 | bytes 4259840 | tf_op jit(solution)/shard_map/reduce_sum | solution.py:76
  70.2 12.1 %add_convert_fusion.2 = bf16[16,16,32,128]{3,2,1,0:T(8,128)(2,1)S(1)} fusion(f32[16,16,32,128]{3,2,1,0:T(8,128)S(1)} %copy-done.2, f32[128]{0:T(128)S(1)} %copy-done.21, f32[16,16,32]{2,1,0:T(8,128)S(1)} %add_rsqrt_fusion.1, f32[16,16,32]{2,1,0:T(8,128)S(1)} %broadcast_multiply_fusion.1, f32[128]{0:T(128)S(1)} %get-tuple-element.40, ...), kind=kLoop, calls=%fused_computation.10 | loop fusion | flops 23068672 | bytes 8687616 | tf_op jit(solution)/shard_map/convert_element_type | solution.py:78
  82.3 0.7 fusion.23
  83.1 0.7 convolution_convert_fusion
  84.4 2.7 %fusion.25 = f32[16,16,32,128]{3,2,1,0:T(8,128)} fusion(bf16[16,16,32,128]{3,2,1,0:T(8,128)(2,1)S(1)} %add_convert_fusion.2, bf16[2,128,128]{2,1,0:T(8,128)(2,1)S(1)} %copy-done.11), kind=kOutput, calls=%fused_computation.113 | convolution fusion | flops 268435456 | bytes 6324224 | tf_op jit(solution)/shard_map/dot_general | solution.py:70
  87.6 1.0 collective-permute-done.6
  88.6 1.4 collective-permute-start.8
  90.1 0.7 collective-permute-start.9
  90.7 1.3 fusion.9
  92.1 1.3 fusion.8
  93.4 1.6 collective-permute-done.8
  95.0 1.6 collective-permute-done.9
  97.0 3.9 %collective-permute-start.11 = (bf16[18,18,1,128]{3,2,1,0:T(2,128)(2,1)S(1)}, bf16[18,18,1,128]{3,2,1,0:T(2,128)(2,1)S(1)}, u32[]{:S(2)}, u32[]{:S(2)}) collective-permute-start(bf16[18,18,1,128]{3,2,1,0:T(2,128)(2,1)S(1)} %get-tuple-element.4), channel_id=1, source_target_pairs={{1,0},{2,1},{3,2},{0,3},{5,4},{6,5},{7,6},{4,7},{9,8},{10,9},{11,1... | collective-permute-start | bytes 248840 | tf_op jit(solution)/shard_map/ppermute | solution.py:18
  100.9 2.9 %fusion.12 = f32[16,16,32,128]{3,2,1,0:T(8,128)} fusion(f32[16,16,32,128]{3,2,1,0:T(8,128)S(1)} %fusion.23, bf16[18,1,32,128]{3,2,1,0:T(8,128)(2,1)S(1)} %collective-permute-done.8, bf16[1,16,32,128]{3,2,1,0:T(8,128)(2,1)S(1)} %collective-permute-done.7, bf16[16,16,32,128]{3,2,1,0:T(8,128)(2,1)S(1)} %convolution_convert_fusion, ...), kind=kOutput, calls=%fused_computation.69 | convolution fusion | flops 279969792 | bytes 10928640 | tf_op jit(solution)/shard_map/dot_general | solution.py:65
  103.8 2.8 %fusion.13 = f32[16,16,32,128]{3,2,1,0:T(8,128)} fusion(f32[16,16,32,128]{3,2,1,0:T(8,128)S(1)} %fusion.23, bf16[18,1,32,128]{3,2,1,0:T(8,128)(2,1)S(1)} %collective-permute-done.9, bf16[1,16,32,128]{3,2,1,0:T(8,128)(2,1)S(1)} %collective-permute-done.7, bf16[16,16,32,128]{3,2,1,0:T(8,128)(2,1)S(1)} %convolution_convert_fusion, ...), kind=kOutput, calls=%fused_computation.70 | convolution fusion | flops 279969792 | bytes 10928640 | tf_op jit(solution)/shard_map/dot_general | solution.py:65
  106.7 4.6 %fusion.15 = f32[16,16,32,128]{3,2,1,0:T(8,128)} fusion(f32[16,16,32,128]{3,2,1,0:T(8,128)S(1)} %fusion.23, bf16[18,18,1,128]{3,2,1,0:T(2,128)(2,1)S(1)} %collective-permute-done.10, bf16[18,1,32,128]{3,2,1,0:T(8,128)(2,1)S(1)} %collective-permute-done.9, bf16[18,1,32,128]{3,2,1,0:T(8,128)(2,1)S(1)} %collective-permute-done.8, ...), kind=kOutput, calls=%fused_computation.72 | convolution fusion | flops 288358400 | bytes 11241984 | tf_op jit(solution)/shard_map/dot_general | solution.py:65
  111.3 8.4 %add_convert_fusion.1 = bf16[16,16,32,128]{3,2,1,0:T(8,128)(2,1)} fusion(f32[16,16,32,128]{3,2,1,0:T(8,128)} %fusion.15, f32[16,16,32,128]{3,2,1,0:T(8,128)} %fusion.13, f32[16,16,32,128]{3,2,1,0:T(8,128)} %fusion.12, f32[16,16,32,128]{3,2,1,0:T(8,128)S(1)} %fusion.8, f32[16,16,32,128]{3,2,1,0:T(8,128)S(1)} %fusion.9, f32[16,16,32,128]{3,2,1,0:T(8,128)S(1)} %fusion.23, ...), kind=kOutput, calls=%fused_computation.3 | convolution fusion | flops 296747008 | bytes 30117376 | tf_op jit(solution)/shard_map/dot_general | solution.py:65
  119.7 6.4 %fusion.102 = (f32[16,16,32]{2,1,0:T(8,128)S(1)}, f32[16,16,32,128]{3,2,1,0:T(8,128)}) fusion(bf16[2,128,128]{2,1,0:T(8,128)(2,1)S(1)} %copy-done.34, f32[16,16,32,128]{3,2,1,0:T(8,128)} %fusion.25, bf16[16,16,32,128]{3,2,1,0:T(8,128)(2,1)} %add_convert_fusion.1, bf16[2,128,128]{2,1,0:T(8,128)(2,1)S(1)} %copy-done.35), kind=kOutput, calls=%fused_computation.210 | convolution fusion | flops 544202752 | bytes 10584064 | tf_op jit(solution)/shard_map/dot_general | solution.py:74
  126.1 4.2 %multiply_reduce_fusion = f32[16,16,32]{2,1,0:T(8,128)S(1)} fusion(f32[16,16,32,128]{3,2,1,0:T(8,128)} %get-tuple-element.47, f32[16,16,32]{2,1,0:T(8,128)S(1)} %broadcast_multiply_fusion), kind=kLoop, calls=%fused_computation.1 | loop fusion | flops 3137536 | bytes 4259840 | tf_op jit(solution)/shard_map/reduce_sum | solution.py:76
  130.3 2.5 %add_convert_fusion = bf16[16,16,32,128]{3,2,1,0:T(8,128)(2,1)S(1)} fusion(bf16[16,16,32,128]{3,2,1,0:T(8,128)(2,1)S(1)} %add_convert_fusion.2, f32[16,16,32,128]{3,2,1,0:T(8,128)S(1)} %copy-done.3, f32[128]{0:T(128)S(1)} %copy-done.20, f32[16,16,32]{2,1,0:T(8,128)S(1)} %add_rsqrt_fusion, f32[16,16,32]{2,1,0:T(8,128)S(1)} %broadcast_multiply_fusion), kind=kLoop, calls=%fused_computation | loop fusion | flops 6291456 | bytes 8454656 | tf_op jit(solution)/shard_map/convert_element_type | solution.py:78
  132.9 1.3 copy-done.5
  134.6 40.8 %all-reduce = (f32[128]{0:T(128)S(1)}, f32[]{:T(128)}) all-reduce(f32[128]{0:T(128)S(1)} %convolution_bitcast_fusion, f32[]{:T(128)} %convert_reduce_fusion), channel_id=1, replica_groups=mesh['gx'=4,'gy'=2,'gz'=4] {'gx','gy','gz'}, use_global_device_ids=true, to_apply=%region_4.5 | all-reduce | flops 129 | bytes 1032 | tf_op jit(solution)/shard_map/psum | solution.py:116
  175.4 1.2 broadcast_divide_fusion
  (101 shorter events, 4.2 us)
Async XLA Ops:
  0.6 11.9 %copy-start.9 = (bf16[2,128,128]{2,1,0:T(8,128)(2,1)S(1)}, bf16[2,128,128]{2,1,0:T(8,128)(2,1)}, u32[]{:S(2)}) copy-start(bf16[2,128,128]{2,1,0:T(8,128)(2,1)} %param.21) | copy-start | bytes 196612
  2.6 10.6 %copy-start.14 = (f32[128]{0:T(128)}, f32[128]{0:T(128)S(1)}, u32[]{:S(2)}) copy-start(f32[128]{0:T(128)S(1)} %get-tuple-element.53) | copy-start | bytes 1540
  2.6 10.6 %copy-start.16 = (f32[128]{0:T(128)}, f32[128]{0:T(128)S(1)}, u32[]{:S(2)}) copy-start(f32[128]{0:T(128)S(1)} %get-tuple-element.54) | copy-start | bytes 1540
  2.6 10.7 %copy-start.18 = (f32[128]{0:T(128)}, f32[128]{0:T(128)S(1)}, u32[]{:S(2)}) copy-start(f32[128]{0:T(128)S(1)} %get-tuple-element.55) | copy-start | bytes 1540
  2.6 15.1 %copy-start.7 = (bf16[2,128,128]{2,1,0:T(8,128)(2,1)S(1)}, bf16[2,128,128]{2,1,0:T(8,128)(2,1)}, u32[]{:S(2)}) copy-start(bf16[2,128,128]{2,1,0:T(8,128)(2,1)} %param.20) | copy-start | bytes 196612
  13.2 1.3 copy-start
  14.6 5.8 %copy-start.13 = (f32[2,6,128]{2,0,1:T(2,128)S(1)}, f32[2,6,128]{2,0,1:T(2,128)}, u32[]{:S(2)}) copy-start(f32[2,6,128]{2,0,1:T(2,128)} %param.22) | copy-start | bytes 18436
  15.2 11.8 %collective-permute-start = (bf16[1,16,32,128]{3,2,1,0:T(8,128)(2,1)}, bf16[1,16,32,128]{3,2,1,0:T(8,128)(2,1)S(1)}, u32[]{:S(2)}, u32[]{:S(2)}) collective-permute-start(bf16[1,16,32,128]{3,2,1,0:T(8,128)(2,1)} %get-tuple-element.14), channel_id=1, source_target_pairs={{0,8},{8,16},{16,24},{24,0},{1,9},{9,17},{17,25},{25,1},{2,10},{10... | collective-permute-start | bytes 393224 | tf_op jit(solution)/shard_map/ppermute | solution.py:15
  15.7 11.3 %collective-permute-start.1 = (bf16[1,16,32,128]{3,2,1,0:T(8,128)(2,1)S(1)}, bf16[1,16,32,128]{3,2,1,0:T(8,128)(2,1)S(1)}, u32[]{:S(2)}, u32[]{:S(2)}) collective-permute-start(bf16[1,16,32,128]{3,2,1,0:T(8,128)(2,1)S(1)} %get-tuple-element.15), channel_id=1, source_target_pairs={{8,0},{16,8},{24,16},{0,24},{9,1},{17,9},{25,17},{1,25},{10,2},{18... | collective-permute-start | bytes 393224 | tf_op jit(solution)/shard_map/ppermute | solution.py:18
  20.3 5.4 %copy-start.6 = (s32[16,16,32]{2,1,0:T(8,128)S(1)}, s32[16,16,32]{2,1,0:T(8,128)}, u32[]{:S(2)}) copy-start(s32[16,16,32]{2,1,0:T(8,128)} %param.17) | copy-start | bytes 98308
  26.4 25.3 %copy-start.36 = (f32[16]{0:T(128)}, f32[16]{0:T(128)S(1)}, u32[]{:S(2)}) copy-start(f32[16]{0:T(128)S(1)} %get-tuple-element.56) | copy-start | bytes 196
  26.4 25.3 %copy-start.38 = (f32[16]{0:T(128)}, f32[16]{0:T(128)S(1)}, u32[]{:S(2)}) copy-start(f32[16]{0:T(128)S(1)} %get-tuple-element.57) | copy-start | bytes 196
  28.1 8.5 %collective-permute-start.2 = (bf16[18,1,32,128]{3,2,1,0:T(8,128)(2,1)S(1)}, bf16[18,1,32,128]{3,2,1,0:T(8,128)(2,1)S(1)}, u32[]{:S(2)}, u32[]{:S(2)}) collective-permute-start(bf16[18,1,32,128]{3,2,1,0:T(8,128)(2,1)S(1)} %get-tuple-element.10), channel_id=1, source_target_pairs={{0,4},{4,0},{1,5},{5,1},{2,6},{6,2},{3,7},{7,3},{8,12},{12,8},{9,1... | collective-permute-start | bytes 442376 | tf_op jit(solution)/shard_map/ppermute | solution.py:15
  30.5 7.3 %collective-permute-start.3 = (bf16[18,1,32,128]{3,2,1,0:T(8,128)(2,1)S(1)}, bf16[18,1,32,128]{3,2,1,0:T(8,128)(2,1)S(1)}, u32[]{:S(2)}, u32[]{:S(2)}) collective-permute-start(bf16[18,1,32,128]{3,2,1,0:T(8,128)(2,1)S(1)} %get-tuple-element.11), channel_id=1, source_target_pairs={{4,0},{0,4},{5,1},{1,5},{6,2},{2,6},{7,3},{3,7},{12,8},{8,12},{13,... | collective-permute-start | bytes 442376 | tf_op jit(solution)/shard_map/ppermute | solution.py:18
  30.6 4.3 %copy-start.1 = (bf16[16,16,32,128]{3,2,1,0:T(8,128)(2,1)S(1)}, bf16[16,16,32,128]{3,2,1,0:T(8,128)(2,1)}, u32[]{:S(2)}) copy-start(bf16[16,16,32,128]{3,2,1,0:T(8,128)(2,1)} %copy-done) | copy-start | bytes 6291460
  30.6 4.7 %copy-start.4 = (f32[16,16,32,128]{3,2,1,0:T(8,128)S(1)}, f32[16,16,32,128]{3,2,1,0:T(8,128)}, u32[]{:S(2)}) copy-start(f32[16,16,32,128]{3,2,1,0:T(8,128)} %fusion.31) | copy-start | bytes 12582916
  30.6 4.7 %copy-start.32 = (f32[128]{0:T(128)S(1)}, f32[128]{0:T(128)}, u32[]{:S(2)}) copy-start(f32[128]{0:T(128)} %get-tuple-element.32) | copy-start | bytes 1540
  30.6 4.7 %copy-start.33 = (bf16[2,128,128]{2,1,0:T(8,128)(2,1)S(1)}, bf16[2,128,128]{2,1,0:T(8,128)(2,1)}, u32[]{:S(2)}) copy-start(bf16[2,128,128]{2,1,0:T(8,128)(2,1)} %param.23) | copy-start | bytes 196612
  35.2 6.7 %copy-start.31 = (f32[128]{0:T(128)S(1)}, f32[128]{0:T(128)}, u32[]{:S(2)}) copy-start(f32[128]{0:T(128)} %get-tuple-element.31) | copy-start | bytes 1540
  38.0 9.0 %collective-permute-start.4 = (bf16[18,18,1,128]{3,2,1,0:T(2,128)(2,1)S(1)}, bf16[18,18,1,128]{3,2,1,0:T(2,128)(2,1)S(1)}, u32[]{:S(2)}, u32[]{:S(2)}) collective-permute-start(bf16[18,18,1,128]{3,2,1,0:T(2,128)(2,1)S(1)} %get-tuple-element.7), channel_id=1, source_target_pairs={{0,1},{1,2},{2,3},{3,0},{4,5},{5,6},{6,7},{7,4},{8,9},{9,10},{10,1... | collective-permute-start | bytes 248840 | tf_op jit(solution)/shard_map/ppermute | solution.py:15
  39.6 12.0 %collective-permute-start.5 = (bf16[18,18,1,128]{3,2,1,0:T(2,128)(2,1)S(1)}, bf16[18,18,1,128]{3,2,1,0:T(2,128)(2,1)S(1)}, u32[]{:S(2)}, u32[]{:S(2)}) collective-permute-start(bf16[18,18,1,128]{3,2,1,0:T(2,128)(2,1)S(1)} %get-tuple-element.6), channel_id=1, source_target_pairs={{1,0},{2,1},{3,2},{0,3},{5,4},{6,5},{7,6},{4,7},{9,8},{10,9},{11,1... | collective-permute-start | bytes 248840 | tf_op jit(solution)/shard_map/ppermute | solution.py:18
  43.2 3.8 %copy-start.29 = (f32[128]{0:T(128)S(1)}, f32[128]{0:T(128)}, u32[]{:S(2)}) copy-start(f32[128]{0:T(128)} %get-tuple-element.29) | copy-start | bytes 1540
  47.0 4.7 %copy-start.28 = (f32[128]{0:T(128)S(1)}, f32[128]{0:T(128)}, u32[]{:S(2)}) copy-start(f32[128]{0:T(128)} %get-tuple-element.28) | copy-start | bytes 1540
  51.7 7.9 %copy-start.34 = (bf16[2,128,128]{2,1,0:T(8,128)(2,1)S(1)}, bf16[2,128,128]{2,1,0:T(8,128)(2,1)}, u32[]{:S(2)}) copy-start(bf16[2,128,128]{2,1,0:T(8,128)(2,1)} %param.26) | copy-start | bytes 196612
  51.7 7.8 %copy-start.35 = (bf16[2,128,128]{2,1,0:T(8,128)(2,1)S(1)}, bf16[2,128,128]{2,1,0:T(8,128)(2,1)}, u32[]{:S(2)}) copy-start(bf16[2,128,128]{2,1,0:T(8,128)(2,1)} %param.25) | copy-start | bytes 196612
  65.9 4.2 %copy-start.2 = (f32[16,16,32,128]{3,2,1,0:T(8,128)S(1)}, f32[16,16,32,128]{3,2,1,0:T(8,128)}, u32[]{:S(2)}) copy-start(f32[16,16,32,128]{3,2,1,0:T(8,128)} %get-tuple-element.45) | copy-start | bytes 12582916
  65.9 4.2 %copy-start.15 = (f32[128]{0:T(128)S(1)}, f32[128]{0:T(128)}, u32[]{:S(2)}) copy-start(f32[128]{0:T(128)} %copy-done.14) | copy-start | bytes 1540
  65.9 4.2 %copy-start.17 = (f32[128]{0:T(128)S(1)}, f32[128]{0:T(128)}, u32[]{:S(2)}) copy-start(f32[128]{0:T(128)} %copy-done.16) | copy-start | bytes 1540
  65.9 4.2 %copy-start.19 = (f32[128]{0:T(128)S(1)}, f32[128]{0:T(128)}, u32[]{:S(2)}) copy-start(f32[128]{0:T(128)} %copy-done.18) | copy-start | bytes 1540
  65.9 4.2 %copy-start.21 = (f32[128]{0:T(128)S(1)}, f32[128]{0:T(128)}, u32[]{:S(2)}) copy-start(f32[128]{0:T(128)} %get-tuple-element.43) | copy-start | bytes 1540
  70.2 12.1 %copy-start.8 = (bf16[2,128,128]{2,1,0:T(8,128)(2,1)S(1)}, bf16[2,128,128]{2,1,0:T(8,128)(2,1)}, u32[]{:S(2)}) copy-start(bf16[2,128,128]{2,1,0:T(8,128)(2,1)} %param.20) | copy-start | bytes 196612
  82.3 2.1 %copy-start.11 = (bf16[2,128,128]{2,1,0:T(8,128)(2,1)S(1)}, bf16[2,128,128]{2,1,0:T(8,128)(2,1)}, u32[]{:S(2)}) copy-start(bf16[2,128,128]{2,1,0:T(8,128)(2,1)} %param.24) | copy-start | bytes 196612
  83.9 3.8 %collective-permute-start.7 = (bf16[1,16,32,128]{3,2,1,0:T(8,128)(2,1)S(1)}, bf16[1,16,32,128]{3,2,1,0:T(8,128)(2,1)S(1)}, u32[]{:S(2)}, u32[]{:S(2)}) collective-permute-start(bf16[1,16,32,128]{3,2,1,0:T(8,128)(2,1)S(1)} %get-tuple-element.13), channel_id=1, source_target_pairs={{8,0},{16,8},{24,16},{0,24},{9,1},{17,9},{25,17},{1,25},{10,2},{18... | collective-permute-start | bytes 393224 | tf_op jit(solution)/shard_map/ppermute | solution.py:18
  83.9 6.8 %copy-start.27 = (f32[128]{0:T(128)S(1)}, f32[128]{0:T(128)}, u32[]{:S(2)}) copy-start(f32[128]{0:T(128)} %get-tuple-element.26) | copy-start | bytes 1540
  83.9 4.7 %collective-permute-start.6 = (bf16[1,16,32,128]{3,2,1,0:T(8,128)(2,1)S(1)}, bf16[1,16,32,128]{3,2,1,0:T(8,128)(2,1)S(1)}, u32[]{:S(2)}, u32[]{:S(2)}) collective-permute-start(bf16[1,16,32,128]{3,2,1,0:T(8,128)(2,1)S(1)} %get-tuple-element.12), channel_id=1, source_target_pairs={{0,8},{8,16},{16,24},{24,0},{1,9},{9,17},{17,25},{25,1},{2,10},{10... | collective-permute-start | bytes 393224 | tf_op jit(solution)/shard_map/ppermute | solution.py:15
  88.6 6.4 %collective-permute-start.8 = (bf16[18,1,32,128]{3,2,1,0:T(8,128)(2,1)S(1)}, bf16[18,1,32,128]{3,2,1,0:T(8,128)(2,1)S(1)}, u32[]{:S(2)}, u32[]{:S(2)}) collective-permute-start(bf16[18,1,32,128]{3,2,1,0:T(8,128)(2,1)S(1)} %get-tuple-element.8), channel_id=1, source_target_pairs={{0,4},{4,0},{1,5},{5,1},{2,6},{6,2},{3,7},{7,3},{8,12},{12,8},{9,1... | collective-permute-start | bytes 442376 | tf_op jit(solution)/shard_map/ppermute | solution.py:15
  90.1 6.5 %collective-permute-start.9 = (bf16[18,1,32,128]{3,2,1,0:T(8,128)(2,1)S(1)}, bf16[18,1,32,128]{3,2,1,0:T(8,128)(2,1)S(1)}, u32[]{:S(2)}, u32[]{:S(2)}) collective-permute-start(bf16[18,1,32,128]{3,2,1,0:T(8,128)(2,1)S(1)} %get-tuple-element.9), channel_id=1, source_target_pairs={{4,0},{0,4},{5,1},{1,5},{6,2},{2,6},{7,3},{3,7},{12,8},{8,12},{13,... | collective-permute-start | bytes 442376 | tf_op jit(solution)/shard_map/ppermute | solution.py:18
  92.0 8.8 %copy-start.25 = (f32[128]{0:T(128)S(1)}, f32[128]{0:T(128)}, u32[]{:S(2)}) copy-start(f32[128]{0:T(128)} %get-tuple-element.25) | copy-start | bytes 1540
  96.8 9.8 %collective-permute-start.10 = (bf16[18,18,1,128]{3,2,1,0:T(2,128)(2,1)S(1)}, bf16[18,18,1,128]{3,2,1,0:T(2,128)(2,1)S(1)}, u32[]{:S(2)}, u32[]{:S(2)}) collective-permute-start(bf16[18,18,1,128]{3,2,1,0:T(2,128)(2,1)S(1)} %get-tuple-element.5), channel_id=1, source_target_pairs={{0,1},{1,2},{2,3},{3,0},{4,5},{5,6},{6,7},{7,4},{8,9},{9,10},{10,1... | collective-permute-start | bytes 248840 | tf_op jit(solution)/shard_map/ppermute | solution.py:15
  97.0 14.2 %collective-permute-start.11 = (bf16[18,18,1,128]{3,2,1,0:T(2,128)(2,1)S(1)}, bf16[18,18,1,128]{3,2,1,0:T(2,128)(2,1)S(1)}, u32[]{:S(2)}, u32[]{:S(2)}) collective-permute-start(bf16[18,18,1,128]{3,2,1,0:T(2,128)(2,1)S(1)} %get-tuple-element.4), channel_id=1, source_target_pairs={{1,0},{2,1},{3,2},{0,3},{5,4},{6,5},{7,6},{4,7},{9,8},{10,9},{11,1... | collective-permute-start | bytes 248840 | tf_op jit(solution)/shard_map/ppermute | solution.py:18
  100.9 3.0 %copy-start.24 = (f32[128]{0:T(128)S(1)}, f32[128]{0:T(128)}, u32[]{:S(2)}) copy-start(f32[128]{0:T(128)} %get-tuple-element.24) | copy-start | bytes 1540
  103.8 2.8 %copy-start.23 = (f32[128]{0:T(128)S(1)}, f32[128]{0:T(128)}, u32[]{:S(2)}) copy-start(f32[128]{0:T(128)} %get-tuple-element.34) | copy-start | bytes 1540
  106.7 4.6 %copy-start.22 = (f32[128]{0:T(128)S(1)}, f32[128]{0:T(128)}, u32[]{:S(2)}) copy-start(f32[128]{0:T(128)} %get-tuple-element.23) | copy-start | bytes 1540
  106.7 4.6 %copy-start.37 = (f32[16]{0:T(128)S(1)}, f32[16]{0:T(128)}, u32[]{:S(2)}) copy-start(f32[16]{0:T(128)} %copy-done.36) | copy-start | bytes 196
  106.7 4.6 %copy-start.39 = (f32[16]{0:T(128)S(1)}, f32[16]{0:T(128)}, u32[]{:S(2)}) copy-start(f32[16]{0:T(128)} %copy-done.38) | copy-start | bytes 196
  126.1 4.2 %copy-start.3 = (f32[16,16,32,128]{3,2,1,0:T(8,128)S(1)}, f32[16,16,32,128]{3,2,1,0:T(8,128)}, u32[]{:S(2)}) copy-start(f32[16,16,32,128]{3,2,1,0:T(8,128)} %get-tuple-element.47) | copy-start | bytes 12582916
  126.1 4.2 %copy-start.20 = (f32[128]{0:T(128)S(1)}, f32[128]{0:T(128)}, u32[]{:S(2)}) copy-start(f32[128]{0:T(128)} %get-tuple-element.42) | copy-start | bytes 1540
  130.3 3.9 %copy-start.12 = (bf16[16,16,32,1]{2,1,0,3:T(8,128)(2,1)S(1)}, bf16[16,16,32,1]{2,1,0,3:T(8,128)(2,1)}, u32[]{:S(2)}) copy-start(bf16[16,16,32,1]{2,1,0,3:T(8,128)(2,1)} %convert_bitcast_fusion) | copy-start | bytes 49156
  (4 other events, 4.8 us)
where the time goes:
time: 177 us
  matrix products  67.7 us (38%)
  blocking collectives  40.8 us (23%)
  other arithmetic  38.1 us (22%)
  starting transfers between devices  15.4 us (9%)
  waiting for transfers between devices  6.8 us (4%)
  local copies, waits for them, and re-layouts  6.76 us (4%)
    dot_general x12, matrix products, update_nodes(): jnp.dot(hidden, edge_out[which_layer], preferred_element_type=jnp.float32)  43.6 us
    psum x1, blocking collectives, per_device(): wall_sum, wall_count = lax.psum((wall_part, count_part), ('gx', 'gy', 'gz'))  40.8 us
    convert_element_type x2, other arithmetic, update_nodes(): return (centre_latent.astype(jnp.float32) + normed).astype(jnp.bfloat16)  14.6 us
    dot_general x2, matrix products, update_nodes(): jnp.dot(inner, node_out[which_layer], preferred_element_type=jnp.float32)  12.8 us
    convert_element_type x1, other arithmetic, per_device(): start_latent = (node_feats.astype(jnp.float32) + lookup(node_type, type_t...  9.89 us
    ppermute x6, starting transfers between devices, with_halo(): lax.ppermute(lax.slice_in_dim(block, 0, width, axis=dim), axis, backward)  8.86 us
    reduce_sum x2, other arithmetic, update_nodes(): spread = jnp.mean(jnp.square(update - centre), axis=-1, keepdims=True)  8.28 us
    ppermute x6, starting transfers between devices, with_halo(): lax.ppermute(lax.slice_in_dim(block, block.shape[dim] - width, None, axis...  6.59 us
  transfers between devices with their start and end apart: 12, of which 6 were waited for; matrix products, arithmetic and copies ran while one was open for 22% of the time, Pallas kernels for 0%

commit v1 on v0

v1 whole, which is shorter than its diff:
```python
import functools

import jax
import jax.numpy as jnp
from jax import lax
from jax.experimental import pallas as pl
from jax.experimental.pallas import tpu as pltpu
from jax.sharding import PartitionSpec as P

epsilon = 1e-05
PAD = 8
F32 = jnp.float32
BF16 = jnp.bfloat16


def dot(a, b):
    return jnp.dot(a, b, preferred_element_type=F32)


def gated(u):
    return u * (1.0 + jnp.tanh(u))


def kernel(
    sizes,
    feats, code, type_table, boundary_table, edge_self, edge_neighbour, edge_bias, edge_out,
    node_self, node_aggregate, node_out, node_gain,
    out, wall_out,
    fbuf, lat, spart, npart, hsum, hbf, table,
    wcat, wnode, wout,
    xsend, xrecv, ysend, yrecv, zsend, zrecv,
    wall, redx, redy, redz,
    fsem, osem, hsend_sem, hrecv_sem, rsend_sem, rrecv_sem,
):
    X, Y, Z, H, L, gx, gy, gz = sizes
    ZP = Z + 2 * PAD
    R = Y * Z
    counts = {"gx": gx, "gy": gy, "gz": gz}
    me = {a: lax.axis_index(a) for a in counts}

    def load_feats(x):
        return pltpu.make_async_copy(feats.at[x], fbuf.at[x], fsem.at[x])

    for x in range(X):
        load_feats(x).start()

    barrier = pltpu.get_barrier_semaphore()
    total = 0
    for a, n in counts.items():
        for k in range(1, n):
            peer = lax.rem(me[a] + k, n)
            pl.semaphore_signal(
                barrier, inc=1, device_id={a: peer}, device_id_type=pl.DeviceIdType.MESH
            )
            total += 1

    for l in range(L):
        wcat[l, :, :H] = (edge_self[l].astype(F32) * 0.5).astype(BF16)
        wcat[l, :, H:] = (edge_neighbour[l].astype(F32) * 0.5).astype(BF16)
        wnode[l, :H] = (node_self[l].astype(F32) * 0.5).astype(BF16)
        wnode[l, H:] = (dot(edge_out[l], node_aggregate[l]) * 0.5).astype(BF16)
        w = node_out[l].astype(F32)
        wout[l] = (w - jnp.mean(w, axis=-1, keepdims=True)).astype(BF16)
    ones = jnp.full((H, H), 1.0 / H, BF16)

    NT, NC = type_table.shape[0], boundary_table.shape[0]
    KT = NT * NC
    KP = table.shape[0]
    table[...] = jnp.zeros_like(table)
    for i in range(NT):
        table[i * NC:(i + 1) * NC] = boundary_table[...] + type_table[i:i + 1]
    t = table[...]
    hi = t.astype(BF16)
    rest = t - hi.astype(F32)
    mid = rest.astype(BF16)
    low = (rest - mid.astype(F32)).astype(BF16)
    table3 = jnp.concatenate([hi, mid, low], axis=0)

    def start_latent(x):
        load_feats(x).wait()
        c = code[x]
        c = jnp.where(c >= KT, c - KT, c)
        rows = lax.broadcasted_iota(jnp.int32, (KP, R), 0)
        hot = jnp.where(rows == c, 1.0, 0.0).astype(BF16)
        hot3 = jnp.concatenate([hot, hot, hot], axis=0)
        extra = lax.dot_general(
            hot3, table3, (((0,), (0,)), ((), ())), preferred_element_type=F32
        )
        lat[x] = (fbuf[x].astype(F32) + extra).astype(BF16)

    def loop(lo, hi, fn):
        def body(i, carry):
            fn(i)
            return carry
        lax.fori_loop(lo, hi, body, 0)

    def halo(l, slot, src, dst, axis, peer):
        return pltpu.make_async_remote_copy(
            src_ref=src,
            dst_ref=dst,
            send_sem=hsend_sem.at[l, slot],
            recv_sem=hrecv_sem.at[l, slot],
            device_id={axis: peer},
            device_id_type=pl.DeviceIdType.MESH,
        )

    up = {a: lax.rem(me[a] + 1, n) for a, n in counts.items()}
    down = {a: lax.rem(me[a] + n - 1, n) for a, n in counts.items()}
    wall[...] = jnp.zeros_like(wall)

    for l in range(L):
        last = l == L - 1
        xs = [
            halo(l, 0, xsend.at[l, 1], xrecv.at[l, 0], "gx", up["gx"]),
            halo(l, 1, xsend.at[l, 0], xrecv.at[l, 1], "gx", down["gx"]),
        ]
        zs = [
            halo(l, 2, zsend.at[l, 1], zrecv.at[l, 0], "gz", up["gz"]),
            halo(l, 3, zsend.at[l, 0], zrecv.at[l, 1], "gz", down["gz"]),
        ]
        y_up = halo(l, 4, ysend.at[l, 1], yrecv.at[l, 0], "gy", up["gy"])
        y_down = halo(l, 5, ysend.at[l, 0], yrecv.at[l, 1], "gy", down["gy"])
        has_low = me["gy"] > 0
        has_high = me["gy"] < gy - 1

        def project(x, face=None, l=l):
            if l == 0:
                start_latent(x)
            p = dot(lat[x], wcat[l])
            spart[x] = p[:, :H]
            n = p[:, H:]
            for y in range(Y):
                npart[x + 1, y * ZP + PAD:y * ZP + PAD + Z] = n[y * Z:(y + 1) * Z]
            if face is not None:
                xsend[l, face] = n.astype(BF16)
            ysend[l, 0, x] = n[:Z].astype(BF16)
            ysend[l, 1, x] = n[R - Z:].astype(BF16)
            zsend[l, 0, x] = npart[x + 1, pl.ds(PAD, Y, stride=ZP), :].astype(BF16)
            zsend[l, 1, x] = npart[x + 1, pl.ds(PAD + Z - 1, Y, stride=ZP), :].astype(BF16)

        project(0, 0)
        project(X - 1, 1)
        if l == 0:
            pl.semaphore_wait(barrier, total)
        for c in xs:
            c.start()
        loop(1, X - 1, project)
        for c in zs:
            c.start()
        pl.when(has_high)(y_up.start)
        pl.when(has_low)(y_down.start)

        bias = [edge_bias[l, d:d + 1] * 0.5 for d in range(6)]

        def neighbour(x, y, dz=0):
            return npart[x, pl.ds(y * ZP + PAD + dz, Z), :]

        def edges_xy(x):
            for y in range(Y):
                s = spart[x, y * Z:(y + 1) * Z]
                h = gated(s + neighbour(x, y) + bias[0]) + gated(s + neighbour(x + 2, y) + bias[1])
                if y > 0:
                    h = h + gated(s + neighbour(x + 1, y - 1) + bias[2])
                if y < Y - 1:
                    h = h + gated(s + neighbour(x + 1, y + 1) + bias[3])
                hsum[x, y * Z:(y + 1) * Z] = h

        loop(1, X - 1, edges_xy)

        for c in xs:
            c.wait()
        for side, slab in ((0, 0), (1, X + 1)):
            for y in range(Y):
                npart[slab, y * ZP + PAD:y * ZP + PAD + Z] = xrecv[l, side, y * Z:(y + 1) * Z].astype(F32)
        loop(0, 2, lambda i: edges_xy(i * (X - 1)))

        @pl.when(has_low)
        def _():
            y_up.wait_recv()

            def add(x):
                s = spart[x, :Z]
                hsum[x, :Z] = hsum[x, :Z] + gated(s + yrecv[l, 0, x].astype(F32) + bias[2])

            loop(0, X, add)

        @pl.when(has_high)
        def _():
            y_down.wait_recv()

            def add(x):
                s = spart[x, R - Z:]
                hsum[x, R - Z:] = hsum[x, R - Z:] + gated(s + yrecv[l, 1, x].astype(F32) + bias[3])

            loop(0, X, add)

        pl.when(has_high)(y_up.wait_send)
        pl.when(has_low)(y_down.wait_send)
        for c in zs:
            c.wait()

        def edges_z(x):
            npart[x + 1, pl.ds(PAD - 1, Y, stride=ZP), :] = zrecv[l, 0, x].astype(F32)
            npart[x + 1, pl.ds(PAD + Z, Y, stride=ZP), :] = zrecv[l, 1, x].astype(F32)
            for y in range(Y):
                rows = slice(y * Z, (y + 1) * Z)
                s = spart[x, rows]
                h = hsum[x, rows]
                h = h + gated(s + neighbour(x + 1, y, -1) + bias[4])
                h = h + gated(s + neighbour(x + 1, y, 1) + bias[5])
                hbf[x, rows] = h.astype(BF16)

        loop(0, X, edges_z)

        gain = node_gain[l:l + 1]

        def store(x):
            return pltpu.make_async_copy(lat.at[x], out.at[x], osem.at[x])

        def nodes(x, l=l, last=last):
            news = []
            B = R // 2
            for b in range(0, R, B):
                old = lat[x, b:b + B]
                u = dot(jnp.concatenate([old, hbf[x, b:b + B]], axis=1), wnode[l])
                inner = gated(u).astype(BF16)
                upd = dot(inner, wout[l])
                var = dot((upd * upd).astype(BF16), ones)
                new = old.astype(F32) + upd * lax.rsqrt(var + epsilon) * gain
                news.append(new.astype(BF16))
            for i, new in enumerate(news):
                lat[x, i * B:(i + 1) * B] = new
            if last:
                store(x).start()
                flag = jnp.where(code[x] >= KT, 1.0, 0.0)
                flag = jnp.broadcast_to(flag, (16, R)).astype(BF16)
                new = jnp.concatenate(news, axis=0)
                wide = jnp.concatenate([new, jnp.ones((R, H), BF16)], axis=1)
                wall[...] += dot(flag, wide)

        loop(0, X, nodes)

    part = wall[:8]
    for index, (a, red) in enumerate((("gx", redx), ("gy", redy), ("gz", redz))):
        n = counts[a]
        red[me[a]] = part
        copies = []
        for k in range(1, n):
            copies.append(pltpu.make_async_remote_copy(
                src_ref=red.at[me[a]],
                dst_ref=red.at[me[a]],
                send_sem=rsend_sem.at[index, k],
                recv_sem=rrecv_sem.at[index, k],
                device_id={a: lax.rem(me[a] + k, n)},
                device_id_type=pl.DeviceIdType.MESH,
            ))
        for c in copies:
            c.start()
        for c in copies:
            c.wait()
        part = red[0]
        for i in range(1, n):
            part = part + red[i]
    wall_out[...] = part[:1, :H] / part[:1, H:]
    loop(0, X, lambda x: store(x).wait())


def per_device(
    node_feats,
    node_type,
    boundary_code,
    wall_flag,
    type_table,
    boundary_table,
    edge_self,
    edge_neighbour,
    edge_bias,
    edge_out,
    node_self,
    node_aggregate,
    node_out,
    node_gain,
):
    X, Y, Z, H = node_feats.shape
    L = edge_self.shape[0]
    gx, gy, gz = (lax.axis_size(a) for a in ("gx", "gy", "gz"))
    NT, NC = type_table.shape[0], boundary_table.shape[0]
    R, ZP = Y * Z, Z + 2 * PAD
    most = max(gx, gy, gz)
    code = (node_type * NC + boundary_code + wall_flag * (NT * NC)).reshape(X, 1, R)
    vmem = pl.BlockSpec(memory_space=pltpu.VMEM)
    hbm = pl.BlockSpec(memory_space=pl.ANY)
    latent, wall_mean = pl.pallas_call(
        functools.partial(kernel, (X, Y, Z, H, L, gx, gy, gz)),
        out_shape=(
            jax.ShapeDtypeStruct((X, R, H), BF16),
            jax.ShapeDtypeStruct((1, H), F32),
        ),
        in_specs=[hbm] + [vmem] * 11,
        out_specs=(hbm, vmem),
        scratch_shapes=[
            pltpu.VMEM((X, R, H), BF16),
            pltpu.VMEM((X, R, H), BF16),
            pltpu.VMEM((X, R, H), F32),
            pltpu.VMEM((X + 2, Y * ZP, H), F32),
            pltpu.VMEM((X, R, H), F32),
            pltpu.VMEM((X, R, H), BF16),
            pltpu.VMEM((pl.cdiv(NT * NC, 16) * 16, H), F32),
            pltpu.VMEM((L, H, 2 * H), BF16),
            pltpu.VMEM((L, 2 * H, H), BF16),
            pltpu.VMEM((L, H, H), BF16),
            pltpu.VMEM((L, 2, R, H), BF16),
            pltpu.VMEM((L, 2, R, H), BF16),
            pltpu.VMEM((L, 2, X, Z, H), BF16),
            pltpu.VMEM((L, 2, X, Z, H), BF16),
            pltpu.VMEM((L, 2, X, Y, H), BF16),
            pltpu.VMEM((L, 2, X, Y, H), BF16),
            pltpu.VMEM((16, 2 * H), F32),
            pltpu.VMEM((gx, 8, 2 * H), F32),
            pltpu.VMEM((gy, 8, 2 * H), F32),
            pltpu.VMEM((gz, 8, 2 * H), F32),
            pltpu.SemaphoreType.DMA((X,)),
            pltpu.SemaphoreType.DMA((X,)),
            pltpu.SemaphoreType.DMA((L, 6)),
            pltpu.SemaphoreType.DMA((L, 6)),
            pltpu.SemaphoreType.DMA((3, most)),
            pltpu.SemaphoreType.DMA((3, most)),
        ],
        compiler_params=pltpu.CompilerParams(collective_id=0, has_side_effects=True),
        name="mesh_step",
    )(
        node_feats.reshape(X, R, H), code, type_table, boundary_table, edge_self, edge_neighbour,
        edge_bias, edge_out, node_self, node_aggregate, node_out, node_gain,
    )
    return latent.reshape(X, Y, Z, H), wall_mean.reshape(H)


def solution(mesh):
    return jax.shard_map(
        per_device,
        mesh=mesh,
        in_specs=(
            P("gx", "gy", "gz", None),
            P("gx", "gy", "gz"),
            P("gx", "gy", "gz"),
            P("gx", "gy", "gz"),
            P(),
            P(),
            P(),
            P(),
            P(),
            P(),
            P(),
            P(),
            P(),
            P(),
        ),
        out_specs=(P("gx", "gy", "gz", None), P()),
        check_vma=False,
    )
```

time: 177 us -> 69.6 us (0.39)
  matrix products: 67.7 us -> 0 us
  Pallas kernels: 0 us -> 61.7 us
  blocking collectives: 40.8 us -> 0 us
  other arithmetic: 38.1 us -> 1.06 us
  starting transfers between devices: 15.4 us -> 0 us
  waiting for transfers between devices: 6.8 us -> 0 us
    dot_general x21 -> x0, matrix products: 67.7 us -> none  [the longest x12 43.6 us: update_nodes(): jnp.dot(hidden, edge_out[which_layer], preferred_element_type=jnp.float32)]
    pallas_call x0 -> x1, Pallas kernels: none -> 61.7 us  [per_device(): pl.pallas_call(functools.partial(kernel, (X, Y, Z, H, L, gx, gy, gz)), ou...]
    psum x1 -> x0, blocking collectives: 40.8 us -> none  [per_device(): wall_sum, wall_count = lax.psum((wall_part, count_part), ('gx', 'gy', 'gz'))]
    convert_element_type x6 -> x0, other arithmetic: 26.2 us -> none  [the longest x2 14.6 us: update_nodes(): return (centre_latent.astype(jnp.float32) + normed).astype(jnp.bfloat16)]
    ppermute x12 -> x0, starting transfers between devices: 15.4 us -> none  [the longest x6 8.86 us: with_halo(): lax.ppermute(lax.slice_in_dim(block, 0, width, axis=dim), axis, backward)]
    reduce_sum x3 -> x0, other arithmetic: 8.98 us -> none  [the longest x2 8.28 us: update_nodes(): spread = jnp.mean(jnp.square(update - centre), axis=-1, keepdims=True)]
    ppermute x12 -> x0, waiting for transfers between devices: 6.8 us -> none  [the longest x6 3.48 us: with_halo(): lax.ppermute(lax.slice_in_dim(block, block.shape[dim] - width, None, axis...]
    mul x2 -> x0, local copies, waits for them, and re-layouts: 2.13 us -> none  [the longest x1 1.29 us: update_nodes(): (update - centre) * lax.rsqrt(spread + epsilon) * node_gain[which_layer]]
  transfers between devices with their start and end apart: 12 -> 0, of which waited for: 6 -> 0; matrix products, arithmetic and copies ran while one was open for 22% -> 0% of each run, Pallas kernels for 0% -> 0%
where the time goes in v1:
time: 69.6 us; the launch traced here: 69.3 us
  Pallas kernels  61.7 us (89%)
  local copies, waits for them, and re-layouts  5.91 us (8%)
  other arithmetic  1.06 us (2%)
    pallas_call x1, Pallas kernels, per_device(): pl.pallas_call(functools.partial(kernel, (X, Y, Z, H, L, gx, gy, gz)), ou...  61.7 us
    unnamed x5, local copies, waits for them, and re-layouts  5.17 us

profile of v1, /device:TPU:0, one launch (start us, length us, event | category | flops | bytes accessed | tf_op | source)
XLA Modules:
  0.0 69.3 jit_solution(174281647636766960)
XLA Ops:
  0.6 1.3 %copy.16.edge_bias = f32[2,6,128]{2,1,0:T(8,128)} copy(f32[2,6,128]{2,0,1:T(2,128)} %param.22) | data formatting | bytes 12288 | tf_op args[8]
  1.9 1.1 %multiply_add_fusion = s32[16,16,32]{2,1,0:T(8,128)S(1)} fusion(s32[16,16,32]{2,1,0:T(8,128)} %param.17, s32[16,16,32]{2,1,0:T(8,128)} %param.16, s32[16,16,32]{2,1,0:T(8,128)} %param.15), kind=kLoop, calls=%fused_computation | loop fusion | flops 32768 | bytes 131072 | tf_op jit(solution)/shard_map/add | solution.py:290
  3.0 0.7 %reshape.17.code = s32[16,1,512]{2,1,0:T(1,128)} reshape(s32[16,16,32]{2,1,0:T(8,128)S(1)} %multiply_add_fusion) | data formatting | bytes 65536 | tf_op jit(solution)/shard_map/reshape | solution.py:290
  3.7 61.7 %mesh_step.1 = (bf16[16,512,128]{2,1,0:T(8,128)(2,1)}, f32[1,128]{1,0:T(1,128)}) custom-call(bf16[16,512,128]{2,1,0:T(8,128)(2,1)} %bitcast.3, s32[16,1,512]{2,1,0:T(1,128)} %reshape.17.code, f32[4,128]{1,0:T(4,128)} %type_table.1, f32[3,128]{1,0:T(4,128)} %boundary_table.1, bf16[2,128,128]{2,1,0:T(8,128)(2,1)} %edge_self.1, ...), custom_call_target="tpu_custom_call" | custom-call | tf_op jit(solution)/shard_map/mesh_step/pallas_call | solution.py:293
  65.4 0.0 copy-start
  65.4 3.4 %copy.19 = bf16[16,16,32,128]{3,2,1,0:T(8,128)(2,1)} copy(bf16[16,16,32,128]{3,2,1,0:T(8,128)(2,1)} %bitcast.4) | data formatting | bytes 4194304
  68.8 0.0 copy-done
  68.8 0.5 copy.20
Async XLA Ops:
  65.4 3.4 %copy-start = (f32[1,128]{1,0:T(1,128)S(1)}, f32[1,128]{1,0:T(1,128)}, u32[]{:S(2)}) copy-start(f32[1,128]{1,0:T(1,128)} %get-tuple-element.5) | copy-start | bytes 1540

commit v2 on v1

--- a/solution.py
+++ b/solution.py
@@ -26,10 +26,10 @@
     feats, code, type_table, boundary_table, edge_self, edge_neighbour, edge_bias, edge_out,
     node_self, node_aggregate, node_out, node_gain,
     out, wall_out,
-    fbuf, lat, spart, npart, hsum, hbf, table,
+    fbuf, lat, spart, npart, hsum, hbf, pre, upd, table,
     wcat, wnode, wout,
     xsend, xrecv, ysend, yrecv, zsend, zrecv,
-    wall, redx, redy, redz,
+    wall, redxy, redz,
     fsem, osem, hsend_sem, hrecv_sem, rsend_sem, rrecv_sem,
 ):
     X, Y, Z, H, L, gx, gy, gz = sizes
@@ -44,15 +44,19 @@
     for x in range(X):
         load_feats(x).start()
 
+    def plane(k):
+        return {"gx": lax.rem(me["gx"] + k // gy, gx), "gy": lax.rem(me["gy"] + k % gy, gy)}
+
+    def line(k):
+        return {"gz": lax.rem(me["gz"] + k, gz)}
+
     barrier = pltpu.get_barrier_semaphore()
-    total = 0
-    for a, n in counts.items():
-        for k in range(1, n):
-            peer = lax.rem(me[a] + k, n)
-            pl.semaphore_signal(
-                barrier, inc=1, device_id={a: peer}, device_id_type=pl.DeviceIdType.MESH
-            )
-            total += 1
+    peers = [plane(k) for k in range(1, gx * gy)] + [line(k) for k in range(1, gz)]
+    total = len(peers)
+    for peer in peers:
+        pl.semaphore_signal(
+            barrier, inc=1, device_id=peer, device_id_type=pl.DeviceIdType.MESH
+        )
 
     for l in range(L):
         wcat[l, :, :H] = (edge_self[l].astype(F32) * 0.5).astype(BF16)
@@ -110,6 +114,8 @@
 
     for l in range(L):
         last = l == L - 1
+        has_low = me["gy"] > 0
+        has_high = me["gy"] < gy - 1
         xs = [
             halo(l, 0, xsend.at[l, 1], xrecv.at[l, 0], "gx", up["gx"]),
             halo(l, 1, xsend.at[l, 0], xrecv.at[l, 1], "gx", down["gx"]),
@@ -120,12 +126,8 @@
         ]
         y_up = halo(l, 4, ysend.at[l, 1], yrecv.at[l, 0], "gy", up["gy"])
         y_down = halo(l, 5, ysend.at[l, 0], yrecv.at[l, 1], "gy", down["gy"])
-        has_low = me["gy"] > 0
-        has_high = me["gy"] < gy - 1
 
         def project(x, face=None, l=l):
-            if l == 0:
-                start_latent(x)
             p = dot(lat[x], wcat[l])
             spart[x] = p[:, :H]
             n = p[:, H:]
@@ -138,35 +140,48 @@
             zsend[l, 0, x] = npart[x + 1, pl.ds(PAD, Y, stride=ZP), :].astype(BF16)
             zsend[l, 1, x] = npart[x + 1, pl.ds(PAD + Z - 1, Y, stride=ZP), :].astype(BF16)
 
-        project(0, 0)
-        project(X - 1, 1)
         if l == 0:
+            start_latent(0)
+
+            def ahead(x):
+                project(x)
+                start_latent(x + 1)
+
+            project(0, 0)
+            start_latent(1)
+            loop(1, X - 1, ahead)
+            project(X - 1, 1)
             pl.semaphore_wait(barrier, total)
-        for c in xs:
-            c.start()
-        loop(1, X - 1, project)
+            for c in xs:
+                c.start()
+        else:
+            project(0, 0)
+            project(X - 1, 1)
+            for c in xs:
+                c.start()
+            loop(1, X - 1, project)
+        pl.when(has_high)(y_up.start)
+        pl.when(has_low)(y_down.start)
         for c in zs:
             c.start()
-        pl.when(has_high)(y_up.start)
-        pl.when(has_low)(y_down.start)
-
-        bias = [edge_bias[l, d:d + 1] * 0.5 for d in range(6)]
+
+        bias = [(edge_bias[d, l:l + 1] * 0.5).astype(BF16) for d in range(6)]
 
         def neighbour(x, y, dz=0):
-            return npart[x, pl.ds(y * ZP + PAD + dz, Z), :]
-
-        def edges_xy(x):
+            return npart[x, pl.ds(y * ZP + PAD + dz, Z), :].astype(BF16)
+
+        def edges_xy(x, l=l, bias=bias):
             for y in range(Y):
-                s = spart[x, y * Z:(y + 1) * Z]
+                rows = slice(y * Z, (y + 1) * Z)
+                s = spart[x, rows].astype(BF16)
                 h = gated(s + neighbour(x, y) + bias[0]) + gated(s + neighbour(x + 2, y) + bias[1])
                 if y > 0:
                     h = h + gated(s + neighbour(x + 1, y - 1) + bias[2])
                 if y < Y - 1:
                     h = h + gated(s + neighbour(x + 1, y + 1) + bias[3])
-                hsum[x, y * Z:(y + 1) * Z] = h
+                hsum[x, rows] = h.astype(F32)
 
         loop(1, X - 1, edges_xy)
-
         for c in xs:
             c.wait()
         for side, slab in ((0, 0), (1, X + 1)):
@@ -174,94 +189,108 @@
                 npart[slab, y * ZP + PAD:y * ZP + PAD + Z] = xrecv[l, side, y * Z:(y + 1) * Z].astype(F32)
         loop(0, 2, lambda i: edges_xy(i * (X - 1)))
 
+        def edge_rows(face, first, d, l=l, bias=bias):
+            def add(x):
+                rows = slice(first, first + Z)
+                u = spart[x, rows] + yrecv[l, face, x].astype(F32) + edge_bias[d, l:l + 1] * 0.5
+                hsum[x, rows] = hsum[x, rows] + gated(u)
+
+            loop(0, X, add)
+
         @pl.when(has_low)
         def _():
             y_up.wait_recv()
-
-            def add(x):
-                s = spart[x, :Z]
-                hsum[x, :Z] = hsum[x, :Z] + gated(s + yrecv[l, 0, x].astype(F32) + bias[2])
-
-            loop(0, X, add)
+            edge_rows(0, 0, 2)
 
         @pl.when(has_high)
         def _():
             y_down.wait_recv()
-
-            def add(x):
-                s = spart[x, R - Z:]
-                hsum[x, R - Z:] = hsum[x, R - Z:] + gated(s + yrecv[l, 1, x].astype(F32) + bias[3])
-
-            loop(0, X, add)
+            edge_rows(1, R - Z, 3)
 
         pl.when(has_high)(y_up.wait_send)
         pl.when(has_low)(y_down.wait_send)
         for c in zs:
             c.wait()
 
-        def edges_z(x):
+        def edges_z(x, l=l, bias=bias):
             npart[x + 1, pl.ds(PAD - 1, Y, stride=ZP), :] = zrecv[l, 0, x].astype(F32)
             npart[x + 1, pl.ds(PAD + Z, Y, stride=ZP), :] = zrecv[l, 1, x].astype(F32)
             for y in range(Y):
                 rows = slice(y * Z, (y + 1) * Z)
-                s = spart[x, rows]
-                h = hsum[x, rows]
-                h = h + gated(s + neighbour(x + 1, y, -1) + bias[4])
+                s = spart[x, rows].astype(BF16)
+                h = gated(s + neighbour(x + 1, y, -1) + bias[4])
                 h = h + gated(s + neighbour(x + 1, y, 1) + bias[5])
-                hbf[x, rows] = h.astype(BF16)
-
-        loop(0, X, edges_z)
+                hbf[x, rows] = h + hsum[x, rows].astype(BF16)
 
         gain = node_gain[l:l + 1]
 
         def store(x):
             return pltpu.make_async_copy(lat.at[x], out.at[x], osem.at[x])
 
-        def nodes(x, l=l, last=last):
-            news = []
-            B = R // 2
-            for b in range(0, R, B):
-                old = lat[x, b:b + B]
-                u = dot(jnp.concatenate([old, hbf[x, b:b + B]], axis=1), wnode[l])
-                inner = gated(u).astype(BF16)
-                upd = dot(inner, wout[l])
-                var = dot((upd * upd).astype(BF16), ones)
-                new = old.astype(F32) + upd * lax.rsqrt(var + epsilon) * gain
-                news.append(new.astype(BF16))
-            for i, new in enumerate(news):
-                lat[x, i * B:(i + 1) * B] = new
+        def first_layer(x, l=l):
+            pre[...] = dot(jnp.concatenate([lat[x], hbf[x]], axis=1), wnode[l])
+
+        def second_layer(l=l):
+            upd[...] = dot(gated(pre[...]).astype(BF16), wout[l])
+
+        def finish(x, last=last, gain=gain):
+            change = upd[...]
+            var = dot((change * change).astype(BF16), ones)
+            new = lat[x].astype(F32) + change * lax.rsqrt(var + epsilon) * gain
+            new = new.astype(BF16)
+            lat[x] = new
             if last:
-                store(x).start()
                 flag = jnp.where(code[x] >= KT, 1.0, 0.0)
                 flag = jnp.broadcast_to(flag, (16, R)).astype(BF16)
-                new = jnp.concatenate(news, axis=0)
                 wide = jnp.concatenate([new, jnp.ones((R, H), BF16)], axis=1)
                 wall[...] += dot(flag, wide)
 
-        loop(0, X, nodes)
-
-    part = wall[:8]
-    for index, (a, red) in enumerate((("gx", redx), ("gy", redy), ("gz", redz))):
-        n = counts[a]
-        red[me[a]] = part
+        def step(x, edge, one, two, three, last=last):
+            if three:
+                finish(x - 3)
+            if two:
+                second_layer()
+            if one:
+                first_layer(x - 1)
+            if edge:
+                edges_z(x)
+            if three and last:
+                store(x - 3).start()
+
+        step(0, True, False, False, False)
+        step(1, True, True, False, False)
+        step(2, True, True, True, False)
+        loop(3, X, lambda x, step=step: step(x, True, True, True, True))
+        step(X, False, True, True, True)
+        step(X + 1, False, False, True, True)
+        step(X + 2, False, False, False, True)
+
+    def exchange(part, red, index, mine, count, place):
+        red[mine] = part
         copies = []
-        for k in range(1, n):
+        for k in range(1, count):
             copies.append(pltpu.make_async_remote_copy(
-                src_ref=red.at[me[a]],
-                dst_ref=red.at[me[a]],
+                src_ref=red.at[mine],
+                dst_ref=red.at[mine],
                 send_sem=rsend_sem.at[index, k],
                 recv_sem=rrecv_sem.at[index, k],
-                device_id={a: lax.rem(me[a] + k, n)},
+                device_id=place(k),
                 device_id_type=pl.DeviceIdType.MESH,
             ))
         for c in copies:
             c.start()
         for c in copies:
             c.wait()
-        part = red[0]
-        for i in range(1, n):
-            part = part + red[i]
-    wall_out[...] = part[:1, :H] / part[:1, H:]
+        total = red[0]
+        for i in range(1, count):
+            total = total + red[i]
+        return total
+
+    first = lax.broadcasted_iota(jnp.int32, (8, H), 0) == 0
+    part = jnp.where(first, wall[:8, :H], wall[:8, H:])
+    part = exchange(part, redxy, 0, me["gx"] * gy + me["gy"], gx * gy, plane)
+    part = exchange(part, redz, 1, me["gz"], gz, line)
+    wall_out[...] = part[:1] / part[1:2]
     loop(0, X, lambda x: store(x).wait())
 
 
@@ -286,7 +315,7 @@
     gx, gy, gz = (lax.axis_size(a) for a in ("gx", "gy", "gz"))
     NT, NC = type_table.shape[0], boundary_table.shape[0]
     R, ZP = Y * Z, Z + 2 * PAD
-    most = max(gx, gy, gz)
+    most = max(gx * gy, gz)
     code = (node_type * NC + boundary_code + wall_flag * (NT * NC)).reshape(X, 1, R)
     vmem = pl.BlockSpec(memory_space=pltpu.VMEM)
     hbm = pl.BlockSpec(memory_space=pl.ANY)
@@ -305,6 +334,8 @@
             pltpu.VMEM((X + 2, Y * ZP, H), F32),
             pltpu.VMEM((X, R, H), F32),
             pltpu.VMEM((X, R, H), BF16),
+            pltpu.VMEM((R, H), F32),
+            pltpu.VMEM((R, H), F32),
             pltpu.VMEM((pl.cdiv(NT * NC, 16) * 16, H), F32),
             pltpu.VMEM((L, H, 2 * H), BF16),
             pltpu.VMEM((L, 2 * H, H), BF16),
@@ -316,21 +347,20 @@
             pltpu.VMEM((L, 2, X, Y, H), BF16),
             pltpu.VMEM((L, 2, X, Y, H), BF16),
             pltpu.VMEM((16, 2 * H), F32),
-            pltpu.VMEM((gx, 8, 2 * H), F32),
-            pltpu.VMEM((gy, 8, 2 * H), F32),
-            pltpu.VMEM((gz, 8, 2 * H), F32),
+            pltpu.VMEM((gx * gy, 8, H), F32),
+            pltpu.VMEM((gz, 8, H), F32),
             pltpu.SemaphoreType.DMA((X,)),
             pltpu.SemaphoreType.DMA((X,)),
             pltpu.SemaphoreType.DMA((L, 6)),
             pltpu.SemaphoreType.DMA((L, 6)),
-            pltpu.SemaphoreType.DMA((3, most)),
-            pltpu.SemaphoreType.DMA((3, most)),
+            pltpu.SemaphoreType.DMA((2, most)),
+            pltpu.SemaphoreType.DMA((2, most)),
         ],
-        compiler_params=pltpu.CompilerParams(collective_id=0, has_side_effects=True),
+        compiler_params=pltpu.CompilerParams(collective_id=0, has_side_effects=True, vmem_limit_bytes=36 * 2**20),
         name="mesh_step",
     )(
         node_feats.reshape(X, R, H), code, type_table, boundary_table, edge_self, edge_neighbour,
-        edge_bias, edge_out, node_self, node_aggregate, node_out, node_gain,
+        jnp.transpose(edge_bias, (1, 0, 2)), edge_out, node_self, node_aggregate, node_out, node_gain,
     )
     return latent.reshape(X, Y, Z, H), wall_mean.reshape(H)
 

time: 69.6 us -> 66.5 us (0.955)
  Pallas kernels: 61.7 us -> 52.9 us
  local copies, waits for them, and re-layouts: 5.91 us -> 11.3 us
    pallas_call x1, Pallas kernels: 61.7 us -> 52.9 us  [per_device(): pl.pallas_call(functools.partial(kernel, (X, Y, Z, H, L, gx, gy, gz)), ou...]
    unnamed x5 -> x24, local copies, waits for them, and re-layouts: 5.17 us -> 11.2 us
where the time goes in v2:
time: 66.5 us; the launch traced here: 65.9 us
  Pallas kernels  52.9 us (80%)
  local copies, waits for them, and re-layouts  11.3 us (17%)
  other arithmetic  1.06 us (2%)
  between operations  0.67 us (1%)
    pallas_call x1, Pallas kernels, per_device(): pl.pallas_call(functools.partial(kernel, (X, Y, Z, H, L, gx, gy, gz)), ou...  52.9 us
    unnamed x24, local copies, waits for them, and re-layouts  11.2 us

profile of v2, /device:TPU:0, one launch (start us, length us, event | category | flops | bytes accessed | tf_op | source)
XLA Modules:
  0.0 65.9 jit_solution(17783984383960267805)
XLA Ops:
  0.6 1.1 %multiply_add_fusion = s32[16,16,32]{2,1,0:T(8,128)S(1)} fusion(s32[16,16,32]{2,1,0:T(8,128)} %param.17, s32[16,16,32]{2,1,0:T(8,128)} %param.16, s32[16,16,32]{2,1,0:T(8,128)} %param.15), kind=kLoop, calls=%fused_computation | loop fusion | flops 32768 | bytes 131072 | tf_op jit(solution)/shard_map/add | solution.py:319
  1.7 0.1 reshape.17.code
  1.8 0.0 copy-start
  1.8 1.6 %copy-done = bf16[16,16,32,128]{3,2,1,0:T(8,128)(2,1)S(1)} copy-done((bf16[16,16,32,128]{3,2,1,0:T(8,128)(2,1)S(1)}, bf16[16,16,32,128]{3,2,1,0:T(8,128)(2,1)}, u32[]{:S(2)}) %copy-start) | copy-done | bytes 2097176
  3.4 0.0 copy-start.1
  3.4 0.8 %copy-done.1 = bf16[2,128,128]{2,1,0:T(8,128)(2,1)S(1)} copy-done((bf16[2,128,128]{2,1,0:T(8,128)(2,1)S(1)}, bf16[2,128,128]{2,1,0:T(8,128)(2,1)}, u32[]{:S(2)}) %copy-start.1) | copy-done | bytes 65560
  4.2 0.0 copy-start.2
  4.2 0.8 %copy-done.2 = bf16[2,128,128]{2,1,0:T(8,128)(2,1)S(1)} copy-done((bf16[2,128,128]{2,1,0:T(8,128)(2,1)S(1)}, bf16[2,128,128]{2,1,0:T(8,128)(2,1)}, u32[]{:S(2)}) %copy-start.2) | copy-done | bytes 65560
  5.1 0.0 copy-start.3
  5.1 0.8 %copy-done.3 = bf16[2,128,128]{2,1,0:T(8,128)(2,1)S(1)} copy-done((bf16[2,128,128]{2,1,0:T(8,128)(2,1)S(1)}, bf16[2,128,128]{2,1,0:T(8,128)(2,1)}, u32[]{:S(2)}) %copy-start.3) | copy-done | bytes 65560
  5.9 0.0 copy-start.4
  5.9 0.8 %copy-done.4 = bf16[2,128,128]{2,1,0:T(8,128)(2,1)S(1)} copy-done((bf16[2,128,128]{2,1,0:T(8,128)(2,1)S(1)}, bf16[2,128,128]{2,1,0:T(8,128)(2,1)}, u32[]{:S(2)}) %copy-start.4) | copy-done | bytes 65560
  6.8 0.0 copy-start.5
  6.8 0.8 %copy-done.5 = bf16[2,128,128]{2,1,0:T(8,128)(2,1)S(1)} copy-done((bf16[2,128,128]{2,1,0:T(8,128)(2,1)S(1)}, bf16[2,128,128]{2,1,0:T(8,128)(2,1)}, u32[]{:S(2)}) %copy-start.5) | copy-done | bytes 65560
  7.6 0.0 copy-start.6
  7.6 0.8 %copy-done.6 = bf16[2,128,128]{2,1,0:T(8,128)(2,1)S(1)} copy-done((bf16[2,128,128]{2,1,0:T(8,128)(2,1)S(1)}, bf16[2,128,128]{2,1,0:T(8,128)(2,1)}, u32[]{:S(2)}) %copy-start.6) | copy-done | bytes 65560
  8.4 0.0 copy-start.7
  8.4 0.7 %copy-done.7 = f32[2,6,128]{2,0,1:T(2,128)S(1)} copy-done((f32[2,6,128]{2,0,1:T(2,128)S(1)}, f32[2,6,128]{2,0,1:T(2,128)}, u32[]{:S(2)}) %copy-start.7) | copy-done | bytes 6168
  9.1 0.0 copy-start.8
  9.1 0.7 %copy-done.8 = f32[4,128]{1,0:T(4,128)S(1)} copy-done((f32[4,128]{1,0:T(4,128)S(1)}, f32[4,128]{1,0:T(4,128)}, u32[]{:S(2)}) %copy-start.8) | copy-done | bytes 2072
  9.8 0.0 copy-start.9
  9.8 0.7 %copy-done.9 = f32[3,128]{1,0:T(4,128)S(1)} copy-done((f32[3,128]{1,0:T(4,128)S(1)}, f32[3,128]{1,0:T(4,128)}, u32[]{:S(2)}) %copy-start.9) | copy-done | bytes 1560
  10.5 0.0 copy-start.10
  10.5 0.7 %copy-done.10 = f32[2,128]{1,0:T(2,128)S(1)} copy-done((f32[2,128]{1,0:T(2,128)S(1)}, f32[2,128]{1,0:T(2,128)}, u32[]{:S(2)}) %copy-start.10) | copy-done | bytes 1048
  11.2 52.9 %mesh_step.1 = (bf16[16,512,128]{2,1,0:T(8,128)(2,1)S(1)}, f32[1,128]{1,0:T(1,128)S(1)}) custom-call(bf16[16,512,128]{2,1,0:T(8,128)(2,1)S(1)} %bitcast.4, s32[16,1,512]{2,1,0:T(1,128)S(1)} %reshape.17.code, f32[4,128]{1,0:T(4,128)S(1)} %copy-done.8, f32[3,128]{1,0:T(4,128)S(1)} %copy-done.9, bf16[2,128,128]{2,1,0:T(8,128)(2,1)S(1)} %copy-done.1, ...), custom_call_target="tpu_custom_call" | custom-call | tf_op jit(solution)/shard_map/mesh_step/pallas_call | solution.py:322
  64.1 1.3 %copy.18 = bf16[16,16,32,128]{3,2,1,0:T(8,128)(2,1)} copy(bf16[16,16,32,128]{3,2,1,0:T(8,128)(2,1)S(1)} %bitcast.5) | data formatting | bytes 4194304
  65.4 0.5 copy.19
Async XLA Ops:
  1.8 1.6 %copy-start = (bf16[16,16,32,128]{3,2,1,0:T(8,128)(2,1)S(1)}, bf16[16,16,32,128]{3,2,1,0:T(8,128)(2,1)}, u32[]{:S(2)}) copy-start(bf16[16,16,32,128]{3,2,1,0:T(8,128)(2,1)} %param.14) | copy-start | bytes 6291460
  3.4 0.8 %copy-start.1 = (bf16[2,128,128]{2,1,0:T(8,128)(2,1)S(1)}, bf16[2,128,128]{2,1,0:T(8,128)(2,1)}, u32[]{:S(2)}) copy-start(bf16[2,128,128]{2,1,0:T(8,128)(2,1)} %edge_self.1) | copy-start | bytes 196612
  4.2 0.8 %copy-start.2 = (bf16[2,128,128]{2,1,0:T(8,128)(2,1)S(1)}, bf16[2,128,128]{2,1,0:T(8,128)(2,1)}, u32[]{:S(2)}) copy-start(bf16[2,128,128]{2,1,0:T(8,128)(2,1)} %edge_neighbour.1) | copy-start | bytes 196612
  5.1 0.8 %copy-start.3 = (bf16[2,128,128]{2,1,0:T(8,128)(2,1)S(1)}, bf16[2,128,128]{2,1,0:T(8,128)(2,1)}, u32[]{:S(2)}) copy-start(bf16[2,128,128]{2,1,0:T(8,128)(2,1)} %edge_out.1) | copy-start | bytes 196612
  5.9 0.8 %copy-start.4 = (bf16[2,128,128]{2,1,0:T(8,128)(2,1)S(1)}, bf16[2,128,128]{2,1,0:T(8,128)(2,1)}, u32[]{:S(2)}) copy-start(bf16[2,128,128]{2,1,0:T(8,128)(2,1)} %node_self.1) | copy-start | bytes 196612
  6.8 0.8 %copy-start.5 = (bf16[2,128,128]{2,1,0:T(8,128)(2,1)S(1)}, bf16[2,128,128]{2,1,0:T(8,128)(2,1)}, u32[]{:S(2)}) copy-start(bf16[2,128,128]{2,1,0:T(8,128)(2,1)} %node_aggregate.1) | copy-start | bytes 196612
  7.6 0.8 %copy-start.6 = (bf16[2,128,128]{2,1,0:T(8,128)(2,1)S(1)}, bf16[2,128,128]{2,1,0:T(8,128)(2,1)}, u32[]{:S(2)}) copy-start(bf16[2,128,128]{2,1,0:T(8,128)(2,1)} %node_out.1) | copy-start | bytes 196612
  8.4 0.7 %copy-start.7 = (f32[2,6,128]{2,0,1:T(2,128)S(1)}, f32[2,6,128]{2,0,1:T(2,128)}, u32[]{:S(2)}) copy-start(f32[2,6,128]{2,0,1:T(2,128)} %param.22) | copy-start | bytes 18436
  9.1 0.7 %copy-start.8 = (f32[4,128]{1,0:T(4,128)S(1)}, f32[4,128]{1,0:T(4,128)}, u32[]{:S(2)}) copy-start(f32[4,128]{1,0:T(4,128)} %type_table.1) | copy-start | bytes 6148
  9.8 0.7 %copy-start.9 = (f32[3,128]{1,0:T(4,128)S(1)}, f32[3,128]{1,0:T(4,128)}, u32[]{:S(2)}) copy-start(f32[3,128]{1,0:T(4,128)} %boundary_table.1) | copy-start | bytes 4612
  10.5 0.7 %copy-start.10 = (f32[2,128]{1,0:T(2,128)S(1)}, f32[2,128]{1,0:T(2,128)}, u32[]{:S(2)}) copy-start(f32[2,128]{1,0:T(2,128)} %node_gain.1) | copy-start | bytes 3076

commit v3 on v2

--- a/solution.py
+++ b/solution.py
@@ -23,15 +23,20 @@
 
 def kernel(
     sizes,
-    feats, code, type_table, boundary_table, edge_self, edge_neighbour, edge_bias, edge_out,
-    node_self, node_aggregate, node_out, node_gain,
-    out, wall_out,
-    fbuf, lat, spart, npart, hsum, hbf, pre, upd, table,
-    wcat, wnode, wout,
-    xsend, xrecv, ysend, yrecv, zsend, zrecv,
-    wall, redxy, redz,
-    fsem, osem, hsend_sem, hrecv_sem, rsend_sem, rrecv_sem,
+    feats, code, *rest,
 ):
+    far, (out, wall_out), held = rest[:10], rest[10:12], rest[12:22]
+    (
+        fbuf, lat, spart, npart, hsum, hbf, pre, upd, table,
+        wcat, wnode, wout,
+        xsend, xrecv, ysend, yrecv, zsend, zrecv,
+        wall, redxy, redz,
+        fsem, wsem, hsend_sem, hrecv_sem, rsend_sem, rrecv_sem,
+    ) = rest[22:]
+    (
+        type_table, boundary_table, edge_self, edge_neighbour, edge_bias, edge_out,
+        node_self, node_aggregate, node_out, node_gain,
+    ) = held
     X, Y, Z, H, L, gx, gy, gz = sizes
     ZP = Z + 2 * PAD
     R = Y * Z
@@ -41,6 +46,9 @@
     def load_feats(x):
         return pltpu.make_async_copy(feats.at[x], fbuf.at[x], fsem.at[x])
 
+    loads = [pltpu.make_async_copy(far[i], held[i], wsem.at[i]) for i in range(len(far))]
+    for c in loads:
+        c.start()
     for x in range(X):
         load_feats(x).start()
 
@@ -58,6 +66,8 @@
             barrier, inc=1, device_id=peer, device_id_type=pl.DeviceIdType.MESH
         )
 
+    for c in loads:
+        c.wait()
     for l in range(L):
         wcat[l, :, :H] = (edge_self[l].astype(F32) * 0.5).astype(BF16)
         wcat[l, :, H:] = (edge_neighbour[l].astype(F32) * 0.5).astype(BF16)
@@ -224,9 +234,6 @@
 
         gain = node_gain[l:l + 1]
 
-        def store(x):
-            return pltpu.make_async_copy(lat.at[x], out.at[x], osem.at[x])
-
         def first_layer(x, l=l):
             pre[...] = dot(jnp.concatenate([lat[x], hbf[x]], axis=1), wnode[l])
 
@@ -238,14 +245,14 @@
             var = dot((change * change).astype(BF16), ones)
             new = lat[x].astype(F32) + change * lax.rsqrt(var + epsilon) * gain
             new = new.astype(BF16)
-            lat[x] = new
+            (out if last else lat)[x] = new
             if last:
                 flag = jnp.where(code[x] >= KT, 1.0, 0.0)
                 flag = jnp.broadcast_to(flag, (16, R)).astype(BF16)
                 wide = jnp.concatenate([new, jnp.ones((R, H), BF16)], axis=1)
                 wall[...] += dot(flag, wide)
 
-        def step(x, edge, one, two, three, last=last):
+        def step(x, edge, one, two, three):
             if three:
                 finish(x - 3)
             if two:
@@ -254,8 +261,6 @@
                 first_layer(x - 1)
             if edge:
                 edges_z(x)
-            if three and last:
-                store(x - 3).start()
 
         step(0, True, False, False, False)
         step(1, True, True, False, False)
@@ -291,7 +296,6 @@
     part = exchange(part, redxy, 0, me["gx"] * gy + me["gy"], gx * gy, plane)
     part = exchange(part, redz, 1, me["gz"], gz, line)
     wall_out[...] = part[:1] / part[1:2]
-    loop(0, X, lambda x: store(x).wait())
 
 
 def per_device(
@@ -318,16 +322,20 @@
     most = max(gx * gy, gz)
     code = (node_type * NC + boundary_code + wall_flag * (NT * NC)).reshape(X, 1, R)
     vmem = pl.BlockSpec(memory_space=pltpu.VMEM)
-    hbm = pl.BlockSpec(memory_space=pl.ANY)
+    hbm = pl.BlockSpec(memory_space=pltpu.HBM)
+    weights = (
+        type_table, boundary_table, edge_self, edge_neighbour, jnp.transpose(edge_bias, (1, 0, 2)),
+        edge_out, node_self, node_aggregate, node_out, node_gain,
+    )
     latent, wall_mean = pl.pallas_call(
         functools.partial(kernel, (X, Y, Z, H, L, gx, gy, gz)),
         out_shape=(
             jax.ShapeDtypeStruct((X, R, H), BF16),
             jax.ShapeDtypeStruct((1, H), F32),
         ),
-        in_specs=[hbm] + [vmem] * 11,
-        out_specs=(hbm, vmem),
-        scratch_shapes=[
+        in_specs=[hbm, vmem] + [hbm] * 10,
+        out_specs=(vmem, vmem),
+        scratch_shapes=[pltpu.VMEM(w.shape, w.dtype) for w in weights] + [
             pltpu.VMEM((X, R, H), BF16),
             pltpu.VMEM((X, R, H), BF16),
             pltpu.VMEM((X, R, H), F32),
@@ -350,17 +358,16 @@
             pltpu.VMEM((gx * gy, 8, H), F32),
             pltpu.VMEM((gz, 8, H), F32),
             pltpu.SemaphoreType.DMA((X,)),
-            pltpu.SemaphoreType.DMA((X,)),
+            pltpu.SemaphoreType.DMA((10,)),
             pltpu.SemaphoreType.DMA((L, 6)),
             pltpu.SemaphoreType.DMA((L, 6)),
             pltpu.SemaphoreType.DMA((2, most)),
             pltpu.SemaphoreType.DMA((2, most)),
         ],
-        compiler_params=pltpu.CompilerParams(collective_id=0, has_side_effects=True, vmem_limit_bytes=36 * 2**20),
+        compiler_params=pltpu.CompilerParams(collective_id=0, has_side_effects=True),
         name="mesh_step",
     )(
-        node_feats.reshape(X, R, H), code, type_table, boundary_table, edge_self, edge_neighbour,
-        jnp.transpose(edge_bias, (1, 0, 2)), edge_out, node_self, node_aggregate, node_out, node_gain,
+        node_feats.reshape(X, R, H), code, *weights,
     )
     return latent.reshape(X, Y, Z, H), wall_mean.reshape(H)
 

time: 66.5 us -> 57.8 us (0.87)
  local copies, waits for them, and re-layouts: 11.3 us -> 4.62 us
  Pallas kernels: 52.9 us -> 51.2 us
    unnamed x24 -> x4, local copies, waits for them, and re-layouts: 11.2 us -> 3.89 us
    pallas_call x1, Pallas kernels: 52.9 us -> 51.2 us  [per_device(): pl.pallas_call(functools.partial(kernel, (X, Y, Z, H, L, gx, gy, gz)), ou...]
where the time goes in v3:
time: 57.8 us; the launch traced here: 57.5 us
  Pallas kernels  51.2 us (89%)
  local copies, waits for them, and re-layouts  4.62 us (8%)
  other arithmetic  1.06 us (2%)
  between operations  0.65 us (1%)
    pallas_call x1, Pallas kernels, per_device(): pl.pallas_call(functools.partial(kernel, (X, Y, Z, H, L, gx, gy, gz)), ou...  51.2 us
    unnamed x4, local copies, waits for them, and re-layouts  3.89 us

profile of v3, /device:TPU:0, one launch (start us, length us, event | category | flops | bytes accessed | tf_op | source)
XLA Modules:
  0.0 57.5 jit_solution(10881817426329064615)
XLA Ops:
  0.6 1.1 %multiply_add_fusion = s32[16,16,32]{2,1,0:T(8,128)S(1)} fusion(s32[16,16,32]{2,1,0:T(8,128)} %param.17, s32[16,16,32]{2,1,0:T(8,128)} %param.16, s32[16,16,32]{2,1,0:T(8,128)} %param.15), kind=kLoop, calls=%fused_computation | loop fusion | flops 32768 | bytes 131072 | tf_op jit(solution)/shard_map/add | solution.py:323
  1.7 0.7 %reshape.17.code = s32[16,1,512]{2,1,0:T(1,128)} reshape(s32[16,16,32]{2,1,0:T(8,128)S(1)} %multiply_add_fusion) | data formatting | bytes 65536 | tf_op jit(solution)/shard_map/reshape | solution.py:323
  2.4 51.2 %mesh_step.1 = (bf16[16,512,128]{2,1,0:T(8,128)(2,1)}, f32[1,128]{1,0:T(1,128)}) custom-call(bf16[16,512,128]{2,1,0:T(8,128)(2,1)} %bitcast.4, s32[16,1,512]{2,1,0:T(1,128)} %reshape.17.code, f32[4,128]{1,0:T(4,128)} %rest_0_.1, f32[3,128]{1,0:T(4,128)} %rest_1_.1, bf16[2,128,128]{2,1,0:T(8,128)(2,1)} %rest_2_.1, bf16[2,128,128]{2,1,0:T(8,128)(2,1)} %rest_3_.1, ...), custom_call_target="tpu_custom_call" | custom-call | tf_op jit(solution)/shard_map/mesh_step/pallas_call | solution.py:330
  53.6 0.0 copy-start
  53.6 3.4 %copy.18 = bf16[16,16,32,128]{3,2,1,0:T(8,128)(2,1)} copy(bf16[16,16,32,128]{3,2,1,0:T(8,128)(2,1)} %bitcast.5) | data formatting | bytes 4194304
  57.0 0.0 copy-done
  57.0 0.5 copy.19
Async XLA Ops:
  53.6 3.4 %copy-start = (f32[1,128]{1,0:T(1,128)S(1)}, f32[1,128]{1,0:T(1,128)}, u32[]{:S(2)}) copy-start(f32[1,128]{1,0:T(1,128)} %get-tuple-element.5) | copy-start | bytes 1540
